TPU v7x, 32 devices: a whole 2x2x4 slice. The times are simulated.
32 devices in a mesh: fsdp: 16 (over z, y, x), dp: 2 (over core).
Axes of the slice: x: 2, y: 2, z: 4, core: 2. Of those that a mesh axis runs over, the one named last changes fastest.
Arguments:
- normed: bfloat16 [2, 4096, 4096], P(None, ('fsdp', 'dp')), may hold values from -6 to 6
- kv_cotangent: bfloat16 [2, 4096, 512], P(None, ('fsdp', 'dp')), may hold values from -6 to 6
- kv_weight: bfloat16 [4096, 512], P('fsdp'), may hold values from -0.09375 to 0.09375
- main_grad: float32 [4096, 512], P('fsdp'), may hold values from -6 to 6
- owner_order: int32 [16], replicated, may hold values from 0 to 15, each once
Outputs:
- key_rows: bfloat16 [2, 4096, 512], P(None, ('fsdp', 'dp'))
- input_grad: bfloat16 [2, 4096, 4096], P(None, ('fsdp', 'dp'))
- grad_buffer: float32 [4096, 512], P('fsdp')
Inputs may be any that keep to these rules, and one draw needn't show every extreme that they name: `owner_order`: a permutation: each value appears once.
All inputs are finite; a program needn't handle non-finite values.
Results may differ from a plain program's by a relative error of at most 0.0075.
Values may be sent and summed in bfloat16 or wider, within the bound.
A program may use at most 64 MiB of HBM per device.

v0:
```python
import functools
import math

import jax
import jax.numpy as jnp
from jax import lax
from jax.experimental import pallas as pl
from jax.experimental.pallas import tpu as pltpu
from jax.sharding import PartitionSpec as P

MESH = pl.DeviceIdType.MESH
F32 = jnp.float32
BF16 = jnp.bfloat16


def kernel(
    n, dp, chunk, scale,
    x_hbm, c_hbm, w_hbm, main_hbm,
    key_hbm, ig_hbm, gb_hbm,
    xx, cc, ck, gath, part, r1, t1, r2, t2, r3, fin, main, gb, key, ig, acc,
    load_sem, out_sem, send_sem, x_recv, az_recv, a1_recv, a2_recv, ad_recv, r1_recv, r2_recv, r3_recv, rd_recv,
):
    f = lax.axis_index("fsdp")
    d = lax.axis_index("dp")
    k = lax.rem(d, 2)
    sib = d + 1 - 2 * k
    rows, width = x_hbm.shape
    key_width = c_hbm.shape[1]
    half = key_width // 2
    depth = n // 4
    chunks = width // chunk
    z = lax.div(f, 4)
    low = lax.rem(f, 4)
    bit0 = lax.rem(low, 2)
    bit1 = lax.div(low, 2)
    flip_x = low + 1 - 2 * bit0
    flip_y = low + 2 - 4 * bit1
    low1 = flip_x + k * (flip_y - flip_x)
    low2 = flip_y + k * (flip_x - flip_y)
    low12 = 3 - low
    p1 = z * 4 + low1
    p2 = z * 4 + low2
    steps = sorted(range(1, depth), key=lambda s: (min(s, depth - s), s))

    def peer(s):
        return lax.rem(z + s, depth)

    def dev(fi, di):
        return {"fsdp": fi, "dp": di}

    loads = []

    def load(src, dst, i):
        cp = pltpu.make_async_copy(src, dst, load_sem.at[i])
        cp.start()
        loads.append(cp)

    load(w_hbm.at[:, pl.ds(0, half)], gath.at[0, f], 0)
    load(w_hbm.at[:, pl.ds(half, half)], gath.at[1, f], 1)
    load(c_hbm, cc.at[0], 2)
    load(x_hbm, xx.at[0], 3)
    load(main_hbm, main, 4)

    barrier = pltpu.get_barrier_semaphore()
    greeted = [dev(peer(s) * 4 + low, d) for s in steps]
    greeted += [dev(p1, d), dev(p2, d)]
    greeted += [dev(f, lax.rem(d + s, dp)) for s in range(1, dp)]
    for g in greeted:
        pl.semaphore_signal(barrier, inc=1, device_id=g, device_id_type=MESH)
    pl.semaphore_wait(barrier, len(greeted))

    sent = []

    def send(src, dst, rsem, to):
        cp = pltpu.make_async_remote_copy(
            src_ref=src, dst_ref=dst, send_sem=send_sem, recv_sem=rsem, device_id=to, device_id_type=MESH
        )
        cp.start()
        sent.append(cp)

    def arrived(dst, rsem, frm):
        pltpu.make_async_remote_copy(
            src_ref=dst, dst_ref=dst, send_sem=send_sem, recv_sem=rsem, device_id=frm, device_id_type=MESH
        ).wait_recv()

    to_sib = dev(f, sib)
    to1 = dev(p1, d)
    to2 = dev(p2, d)

    send(x_hbm, xx.at[1], x_recv.at[0], to_sib)
    send(c_hbm, cc.at[1], x_recv.at[1], to_sib)
    loads[0].wait()
    loads[1].wait()

    def block(fi):
        return gath.at[k, fi]

    send(block(f), block(f), a1_recv.at[z], to1)
    send(block(f), block(f), a2_recv.at[z], to2)
    for s in steps:
        send(block(f), block(f), az_recv.at[z], dev(peer(s) * 4 + low, d))

    loads[2].wait()
    loads[3].wait()
    arrived(cc.at[1], x_recv.at[1], to_sib)
    arrived(xx.at[1], x_recv.at[0], to_sib)
    side = pl.ds(pl.multiple_of(k * half, half), half)
    ck[...] = cc[:, :, side].reshape(2 * rows, half)

    per = chunk // part.shape[1]
    ring = steps + [0]
    blockwise = per == 1

    def partial(cols):
        both = xx[:, :, cols].reshape(2 * rows, chunk)
        prod = lax.dot_general(both, ck[...], (((0,), (0,)), ((), ())), preferred_element_type=F32)
        return prod.astype(BF16)

    def feature_block(fb):
        return pl.ds(pl.multiple_of(fb * chunk, chunk), chunk)

    def partials(lo):
        if blockwise:
            for s in ring:
                fb = peer(s) * 4 + lo
                part[fb] = partial(feature_block(fb))
                if lo is low12:
                    send(part.at[fb], r1.at[0, peer(s)], r1_recv.at[0, peer(s)], to1)
                if lo is low1:
                    send(part.at[fb], r1.at[1, peer(s)], r1_recv.at[1, peer(s)], to1)

    if not blockwise:
        for j in range(chunks):
            made = partial(pl.ds(j * chunk, chunk))
            part[j * per : (j + 1) * per] = made.reshape(per, part.shape[1], half)
        for s in ring:
            send(part.at[peer(s) * 4 + low12], r1.at[0, peer(s)], r1_recv.at[0, peer(s)], to1)
    partials(low12)
    for s in steps:
        zb = peer(s)
        fb = zb * 4 + low
        arrived(block(fb), az_recv.at[zb], dev(fb, d))
        send(block(fb), block(fb), a1_recv.at[zb], to1)
        send(block(fb), block(fb), a2_recv.at[zb], to2)
        send(block(fb), block(fb), ad_recv.at[fb], to_sib)
    if not blockwise:
        for s in ring:
            send(part.at[peer(s) * 4 + low1], r1.at[1, peer(s)], r1_recv.at[1, peer(s)], to1)
    partials(low1)
    partials(low2)
    partials(low)

    outs = []

    def put(src, dst, i):
        cp = pltpu.make_async_copy(src, dst, out_sem.at[i])
        cp.start()
        outs.append(cp)

    contract = (((1,), (1,)), ((), ()))

    def from_sib(lo):
        for s in [0] + steps:
            fb = peer(s) * 4 + lo
            if s or lo is not low:
                arrived(gath.at[1 - k, fb], ad_recv.at[fb], to_sib)

    def use(lo):
        if not blockwise:
            return
        from_sib(lo)
        for s in [0] + steps:
            fb = peer(s) * 4 + lo
            cols = feature_block(fb)
            w0 = gath[0, fb]
            w1 = gath[1, fb]
            prod = lax.dot_general(cc[0, :, :half], w0, contract, preferred_element_type=F32)
            prod = prod + lax.dot_general(cc[0, :, half:], w1, contract, preferred_element_type=F32)
            ig[:, cols] = prod.astype(BF16)
            put(ig.at[:, cols], ig_hbm.at[:, cols], len(outs))
            xb = xx[0, :, cols]
            k0 = jnp.dot(xb, w0, preferred_element_type=F32)
            k1 = jnp.dot(xb, w1, preferred_element_type=F32)
            if s == 0 and lo is low:
                acc[:, :half] = k0
                acc[:, half:] = k1
            else:
                acc[:, :half] += k0
                acc[:, half:] += k1

    for s in [0] + steps:
        zb = peer(s)
        fb = zb * 4 + low1
        arrived(block(fb), a1_recv.at[zb], to1)
        send(block(fb), block(fb), a2_recv.at[depth + zb], to2)
        send(block(fb), block(fb), ad_recv.at[fb], to_sib)
    for s in ring:
        zb = peer(s)
        arrived(r1.at[0, zb], r1_recv.at[0, zb], to1)
        t1[zb] = (part[zb * 4 + low2].astype(F32) + r1[0, zb].astype(F32)).astype(BF16)
        send(t1.at[zb], r2.at[zb], r2_recv.at[zb], to2)
    use(low)
    for s in steps:
        zb = peer(s)
        arrived(r1.at[1, zb], r1_recv.at[1, zb], to1)
        arrived(r2.at[zb], r2_recv.at[zb], to2)
        t2[zb] = (part[zb * 4 + low].astype(F32) + r1[1, zb].astype(F32) + r2[zb].astype(F32)).astype(BF16)
        send(t2.at[zb], r3.at[z], r3_recv.at[z], dev(zb * 4 + low, d))
    for s in [0] + steps:
        zb = peer(s)
        fb = zb * 4 + low2
        arrived(block(fb), a2_recv.at[zb], to2)
        send(block(fb), block(fb), ad_recv.at[fb], to_sib)
    use(low1)
    use(low2)
    for s in [0] + steps:
        zb = peer(s)
        fb = zb * 4 + low12
        arrived(block(fb), a2_recv.at[depth + zb], to2)
        send(block(fb), block(fb), ad_recv.at[fb], to_sib)

    arrived(r1.at[1, z], r1_recv.at[1, z], to1)
    arrived(r2.at[z], r2_recv.at[z], to2)
    total = part[f].astype(F32) + r1[1, z].astype(F32) + r2[z].astype(F32)
    for s in steps:
        arrived(r3.at[peer(s)], r3_recv.at[peer(s)], dev(peer(s) * 4 + low, d))
        total = total + r3[peer(s)].astype(F32)
    fin[d] = total
    for s in range(1, dp):
        send(fin.at[d], fin.at[d], rd_recv.at[d], dev(f, lax.rem(d + s, dp)))

    use(low12)
    if blockwise:
        key[...] = acc[...].astype(BF16)
    else:
        for lo in (low, low1, low2, low12):
            from_sib(lo)
        for j in range(chunks):
            w0 = gath[0, j * per : (j + 1) * per].reshape(chunk, half)
            w1 = gath[1, j * per : (j + 1) * per].reshape(chunk, half)
            prod = lax.dot_general(cc[0, :, :half], w0, contract, preferred_element_type=F32)
            prod = prod + lax.dot_general(cc[0, :, half:], w1, contract, preferred_element_type=F32)
            ig[:, j * chunk : (j + 1) * chunk] = prod.astype(BF16)
        put(ig, ig_hbm, 0)
        for h in range(2):
            w = gath[h].reshape(width, half)
            key[:, h * half : (h + 1) * half] = jnp.dot(xx[0], w, preferred_element_type=F32).astype(BF16)
    put(key, key_hbm, len(outs))

    for s in range(1, dp):
        src = lax.rem(d + s, dp)
        arrived(fin.at[src], rd_recv.at[src], dev(f, src))
    loads[4].wait()
    for h in range(2):
        total = fin[h]
        for g in range(1, dp // 2):
            total = total + fin[2 * g + h]
        cols = slice(h * half, (h + 1) * half)
        gb[:, cols] = main[:, cols] + total * scale
    put(gb, gb_hbm, len(outs))
    for cp in sent:
        cp.wait_send()
    for cp in outs:
        cp.wait()


def reorder_kernel(depth, scatter, order_ref, x_ref, y_ref):
    for j in range(x_ref.shape[1] // depth):
        here = slice(j * depth, (j + 1) * depth)
        there = pl.ds(pl.multiple_of(order_ref[j] * depth, depth), depth)
        if scatter:
            y_ref[:, there] = x_ref[:, here]
        else:
            y_ref[:, here] = x_ref[:, there]


def reorder(x, order, scatter):
    rows, width = x.shape
    n = order.shape[0]
    depth = width // n
    if depth % 128:
        if scatter:
            order = jnp.argsort(order)
        return jnp.take(x.reshape(rows, n, depth), order, axis=1, mode="clip").reshape(rows, width)
    tile = rows // 4
    spec = pl.BlockSpec((tile, width), lambda i: (i, 0))
    return pl.pallas_call(
        functools.partial(reorder_kernel, depth, scatter),
        grid=(rows // tile,),
        out_shape=jax.ShapeDtypeStruct((rows, width), x.dtype),
        in_specs=[pl.BlockSpec(memory_space=pltpu.SMEM), spec],
        out_specs=spec,
        cost_estimate=pl.CostEstimate(flops=0, bytes_accessed=4 * rows * width, transcendentals=0),
    )(order, x)


def body(normed, kv_cotangent, kv_weight, main_grad, owner_order):
    micro_count, tok_dev, width = normed.shape
    shard_rows, key_width = kv_weight.shape
    n = lax.axis_size("fsdp")
    dp = lax.axis_size("dp")
    rows = micro_count * tok_dev
    half = key_width // 2
    depth = n // 4
    scale = 1.0 / math.sqrt(rows * n * dp)
    chunk = shard_rows if shard_rows % 128 == 0 else max(shard_rows, 256)
    x = reorder(normed.reshape(rows, width), owner_order, False)
    chunks = width // chunk
    dma = pltpu.SemaphoreType.DMA
    half_block = (shard_rows, half)
    any_spec = pl.BlockSpec(memory_space=pl.ANY)
    key, ig, gb = pl.pallas_call(
        functools.partial(kernel, n, dp, chunk, scale),
        out_shape=(
            jax.ShapeDtypeStruct((rows, key_width), BF16),
            jax.ShapeDtypeStruct((rows, width), BF16),
            jax.ShapeDtypeStruct((shard_rows, key_width), F32),
        ),
        in_specs=[any_spec] * 4,
        out_specs=(any_spec,) * 3,
        scratch_shapes=[
            pltpu.VMEM((2, rows, width), BF16),
            pltpu.VMEM((2, rows, key_width), BF16),
            pltpu.VMEM((2 * rows, half), BF16),
            pltpu.VMEM((2, n) + half_block, BF16),
            pltpu.VMEM((n,) + half_block, BF16),
            pltpu.VMEM((2, depth) + half_block, BF16),
            pltpu.VMEM((depth,) + half_block, BF16),
            pltpu.VMEM((depth,) + half_block, BF16),
            pltpu.VMEM((depth,) + half_block, BF16),
            pltpu.VMEM((depth,) + half_block, BF16),
            pltpu.VMEM((dp,) + half_block, F32),
            pltpu.VMEM((shard_rows, key_width), F32),
            pltpu.VMEM((shard_rows, key_width), F32),
            pltpu.VMEM((rows, key_width), BF16),
            pltpu.VMEM((rows, width), BF16),
            pltpu.VMEM((rows, key_width), F32),
            dma((5,)),
            dma((chunks + 2,)),
            dma,
            dma((2,)),
            dma((depth,)),
            dma((depth,)),
            dma((2 * depth,)),
            dma((n,)),
            dma((2, depth)),
            dma((depth,)),
            dma((depth,)),
            dma((dp,)),
        ],
        compiler_params=pltpu.CompilerParams(
            collective_id=0, has_side_effects=True
        ),
    )(x, kv_cotangent.reshape(rows, key_width), kv_weight, main_grad)
    ig = reorder(ig, owner_order, True)
    return (
        key.reshape(micro_count, tok_dev, key_width),
        ig.reshape(micro_count, tok_dev, width),
        gb,
    )


def solution(mesh):
    in_specs = (
        P(None, ("fsdp", "dp"), None),
        P(None, ("fsdp", "dp"), None),
        P("fsdp", None),
        P("fsdp", None),
        P(),
    )
    out_specs = (P(None, ("fsdp", "dp"), None), P(None, ("fsdp", "dp"), None), P("fsdp", None))
    return jax.shard_map(body, mesh=mesh, in_specs=in_specs, out_specs=out_specs, check_vma=False)
```

profile of v0, /device:TPU:1, one launch (start us, length us, event | category | flops | bytes accessed | tf_op | source)
XLA Modules:
  0.0 63.5 jit_solution(15236538689039537021)
XLA Ops:
  0.6 3.9 %shard_map.76.x_hbm = bf16[256,4096]{1,0:T(8,128)(2,1)} custom-call(s32[16]{0:T(128)} %order_ref.3, bf16[256,4096]{1,0:T(8,128)(2,1)} %bitcast.4), custom_call_target="tpu_custom_call" | custom-call | bytes 4194304 | tf_op jit(solution)/shard_map/pallas_call | solution.py:287
  4.5 53.6 %shard_map.77 = (bf16[256,512]{1,0:T(8,128)(2,1)}, bf16[256,4096]{1,0:T(8,128)(2,1)}, f32[256,512]{1,0:T(8,128)}) custom-call(bf16[256,4096]{1,0:T(8,128)(2,1)} %shard_map.76.x_hbm, bf16[256,512]{1,0:T(8,128)(2,1)} %bitcast.6, bf16[256,512]{1,0:T(8,128)(2,1)} %w_hbm.1, f32[256,512]{1,0:T(8,128)} %main_hbm.1), custom_call_target="tpu_custom_call" | custom-call | tf_op jit(solution)/shard_map/pallas_call | solution.py:312
  58.1 0.0 copy-start.1
  58.1 0.0 copy-start
  58.1 3.9 %shard_map.78 = bf16[256,4096]{1,0:T(8,128)(2,1)} custom-call(s32[16]{0:T(128)} %order_ref.3, bf16[256,4096]{1,0:T(8,128)(2,1)} %get-tuple-element.7.x_ref), custom_call_target="tpu_custom_call" | custom-call | bytes 4194304 | tf_op jit(solution)/shard_map/pallas_call | solution.py:287
  62.0 0.0 copy-done.1
  62.0 0.7 %copy.10 = bf16[2,128,512]{2,1,0:T(8,128)(2,1)} copy(bf16[2,128,512]{2,1,0:T(8,128)(2,1)S(1)} %bitcast.7) | data formatting | bytes 524288
  62.7 0.0 copy-done
  62.7 0.8 %copy.11 = f32[256,512]{1,0:T(8,128)} copy(f32[256,512]{1,0:T(8,128)S(1)} %copy-done) | data formatting | bytes 1048576
Async XLA Ops:
  58.1 4.0 %copy-start.1 = (bf16[256,512]{1,0:T(8,128)(2,1)S(1)}, bf16[256,512]{1,0:T(8,128)(2,1)}, u32[]{:S(2)}) copy-start(bf16[256,512]{1,0:T(8,128)(2,1)} %get-tuple-element.6) | copy-start | bytes 786436
  58.1 4.6 %copy-start = (f32[256,512]{1,0:T(8,128)S(1)}, f32[256,512]{1,0:T(8,128)}, u32[]{:S(2)}) copy-start(f32[256,512]{1,0:T(8,128)} %get-tuple-element.14) | copy-start | bytes 1572868
where the time goes:
time: 63.8 us; the launch traced here: 63.5 us
  Pallas kernels  61.4 us (96%)
  local copies, waits for them, and re-layouts  1.5 us (2%)
  between operations  0.66 us (1%)
    pallas_call x1, Pallas kernels, body(): pl.pallas_call(functools.partial(kernel, n, dp, chunk, scale), out_shape=...  53.6 us
    pallas_call x2, Pallas kernels, reorder(): pl.pallas_call(functools.partial(reorder_kernel, depth, scatter), grid=(r...  7.82 us
    unnamed x6, local copies, waits for them, and re-layouts  1.5 us

commit v1 on v0

--- a/solution.py
+++ b/solution.py
@@ -294,6 +294,455 @@
     )(order, x)
 
 
+def exchange(
+    n, dp, scale,
+    order_hbm, x_hbm, c_hbm, w_hbm, main_hbm,
+    key, ig, gb, order,
+    xx, cc, ck, gath, mine, give, take, part, r1, hop, zin, t3, r3, fin, main, acc,
+    load_sem, send_sem, ag_recv, sib_recv, take_recv, r1_recv, z_recv, r3_recv, fin_recv,
+):
+    f = lax.axis_index("fsdp")
+    d = lax.axis_index("dp")
+    k = lax.rem(d, 2)
+    sib = d + 1 - 2 * k
+    chunk, key_width = main_hbm.shape
+    half = key_width // 2
+    depth = n // 4
+    z = lax.div(f, 4)
+    low = lax.rem(f, 4)
+    bit0 = lax.rem(low, 2)
+    bit1 = lax.div(low, 2)
+    flip0 = low + 1 - 2 * bit0
+    flip1 = low + 2 - 4 * bit1
+    low_a = flip0 + k * (flip1 - flip0)
+    low_b = flip1 + k * (flip0 - flip1)
+    low_ab = 3 - low
+    upper = lax.div(2 * z, depth)
+    has_up = z < depth - 1
+    has_dn = z > 0
+    mid = jnp.logical_and(has_up, has_dn)
+
+    def far(t):
+        return (1 - upper) * (depth - 1 - t) + upper * t
+
+    def close(i):
+        up = i + jnp.where(i >= z, 1, 0)
+        dn = depth - 1 - i - jnp.where(depth - 1 - i <= z, 1, 0)
+        return (1 - upper) * up + upper * dn
+
+    def dev(fi, di):
+        return {"fsdp": fi, "dp": di}
+
+    to_a = dev(z * 4 + low_a, d)
+    to_b = dev(z * 4 + low_b, d)
+    to_sib = dev(f, sib)
+
+    def level(zi):
+        return dev(lax.rem(zi + depth, depth) * 4 + low, d)
+
+    loads = []
+
+    def load(src, dst):
+        cp = pltpu.make_async_copy(src, dst, load_sem.at[len(loads)])
+        cp.start()
+        loads.append(cp)
+
+    load(w_hbm.at[:, pl.ds(0, half)], gath.at[0, f])
+    load(w_hbm.at[:, pl.ds(half, half)], gath.at[1, f])
+    load(order_hbm, order)
+    load(c_hbm, cc)
+    for j in range(n):
+        load(x_hbm.at[:, pl.ds(j * chunk, chunk)], xx.at[j])
+    load(main_hbm, main)
+    load_x = loads[4 : 4 + n]
+
+    barrier = pltpu.get_barrier_semaphore()
+
+    def greet(to):
+        pl.semaphore_signal(barrier, inc=1, device_id=to, device_id_type=MESH)
+
+    greet(to_a)
+    greet(to_b)
+    for s in range(1, dp):
+        greet(dev(f, lax.rem(d + s, dp)))
+
+    @pl.when(has_up)
+    def _():
+        greet(level(z + 1))
+
+    @pl.when(has_dn)
+    def _():
+        greet(level(z - 1))
+
+    pl.semaphore_wait(barrier, dp + 1 + jnp.where(has_up, 1, 0) + jnp.where(has_dn, 1, 0))
+
+    sent = []
+
+    def send(src, dst, rsem, to, cond=None):
+        cp = pltpu.make_async_remote_copy(
+            src_ref=src, dst_ref=dst, send_sem=send_sem, recv_sem=rsem, device_id=to, device_id_type=MESH
+        )
+        if cond is None:
+            cp.start()
+        else:
+            pl.when(cond)(cp.start)
+        return cp, cond
+
+    def post(*args):
+        sent.append(send(*args))
+
+    def arrived(dst, rsem):
+        pltpu.make_async_remote_copy(
+            src_ref=dst, dst_ref=dst, send_sem=send_sem, recv_sem=rsem, device_id=to_sib, device_id_type=MESH
+        ).wait_recv()
+
+    def block(fb):
+        return gath.at[k, fb]
+
+    def forward(fb, to, cond=None):
+        send(block(fb), block(fb), ag_recv.at[fb], to, cond)
+
+    def forward_sib(fb):
+        send(block(fb), block(fb), sib_recv.at[fb], to_sib)
+
+    contract_rows = (((0,), (0,)), ((), ()))
+    contract_cols = (((1,), (1,)), ((), ()))
+
+    def partial(lo, t):
+        fb = far(t) * 4 + lo
+        prod = lax.dot_general(xx[order[fb]], ck[...], contract_rows, preferred_element_type=F32)
+        give[fb] = prod[:, half:].astype(BF16)
+        send(give.at[fb], take.at[fb], take_recv.at[fb], to_sib)
+        mine[fb] = prod[:, :half]
+
+    def pair(fb):
+        return mine[fb] + take[fb].astype(F32)
+
+    def across(j, t):
+        zz = far(t)
+        fb = zz * 4 + (low_ab if j else low_b)
+        arrived(take.at[fb], take_recv.at[fb])
+        part[fb] = pair(fb).astype(BF16)
+        send(part.at[fb], r1.at[j, zz], r1_recv.at[j, zz], to_b)
+
+    def from_a():
+        fb = z * 4 + low_a
+        arrived(block(fb), ag_recv.at[fb])
+        forward(fb, level(z + 1), has_up)
+        forward(fb, level(z - 1), has_dn)
+        forward_sib(fb)
+
+    def from_z(i, j):
+        zz = close(i)
+        fb = zz * 4 + (low_a if j else low)
+        arrived(block(fb), ag_recv.at[fb])
+        below = zz < z
+        on = jnp.logical_or(jnp.logical_and(below, has_up), jnp.logical_and(zz > z, has_dn))
+        forward(fb, level(z + jnp.where(below, 1, -1)), on)
+        forward(fb, to_b)
+        forward_sib(fb)
+
+    def from_b(zz, j):
+        fb = zz * 4 + (low_ab if j else low_b)
+        arrived(block(fb), ag_recv.at[fb])
+        forward_sib(fb)
+
+    def ready(j, zz):
+        fb = zz * 4 + (low_a if j else low)
+        arrived(take.at[fb], take_recv.at[fb])
+        arrived(r1.at[j, zz], r1_recv.at[j, zz])
+        return pair(fb) + r1[j, zz].astype(F32)
+
+    def along(t, j):
+        zz = far(t)
+
+        @pl.when(zz != z)
+        def _():
+            side = jnp.where(zz > z, 0, 1)
+            edge = jnp.where(zz > z, z == 0, z == depth - 1)
+
+            @pl.when(jnp.logical_not(edge))
+            def _():
+                arrived(zin.at[side, zz, j], z_recv.at[side, zz, j])
+
+            total = ready(j, zz) + zin[side, zz, j].astype(F32)
+            hop[j, zz] = total.astype(BF16)
+            send(hop.at[j, zz], zin.at[side, zz, j], z_recv.at[side, zz, j], level(z + 1 - 2 * side))
+
+    def settle(j):
+        total = ready(j, z)
+
+        @pl.when(has_dn)
+        def _():
+            arrived(zin.at[0, z, j], z_recv.at[0, z, j])
+
+        @pl.when(has_up)
+        def _():
+            arrived(zin.at[1, z, j], z_recv.at[1, z, j])
+
+        return total + zin[0, z, j].astype(F32) + zin[1, z, j].astype(F32)
+
+    def use(fb, first=False):
+        w0 = gath[0, fb]
+        w1 = gath[1, fb]
+        prod = lax.dot_general(cc[:, :half], w0, contract_cols, preferred_element_type=F32)
+        prod = prod + lax.dot_general(cc[:, half:], w1, contract_cols, preferred_element_type=F32)
+        ig[fb] = prod.astype(BF16)
+        xb = xx[order[fb]]
+        k0 = jnp.dot(xb, w0, preferred_element_type=F32)
+        k1 = jnp.dot(xb, w1, preferred_element_type=F32)
+        if first:
+            acc[:, :half] = k0
+            acc[:, half:] = k1
+        else:
+            acc[:, :half] += k0
+            acc[:, half:] += k1
+
+    def use_when(zz, lo):
+        fb = zz * 4 + lo
+        arrived(gath.at[1 - k, fb], sib_recv.at[fb])
+        use(fb)
+
+    loads[0].wait()
+    loads[1].wait()
+    forward(f, to_a)
+    forward(f, level(z + 1), has_up)
+    forward(f, level(z - 1), has_dn)
+
+    @pl.when(z == 0)
+    def _():
+        zin[0] = jnp.zeros(zin.shape[1:], BF16)
+
+    @pl.when(z == depth - 1)
+    def _():
+        zin[1] = jnp.zeros(zin.shape[1:], BF16)
+
+    loads[3].wait()
+    ck[:, :half] = cc[:, pl.ds(pl.multiple_of(k * half, half), half)]
+    ck[:, half:] = cc[:, pl.ds(pl.multiple_of((1 - k) * half, half), half)]
+    loads[2].wait()
+    for cp in load_x:
+        cp.wait()
+
+    steps = []
+    for t in range(depth):
+        steps += [
+            functools.partial(partial, low_ab, t),
+            functools.partial(partial, low_a, t),
+            functools.partial(partial, low_b, t),
+        ]
+    sends = []
+    for t in range(depth):
+        sends += [functools.partial(across, 1, t), functools.partial(across, 0, t)]
+    LAG = 3
+    due = {}
+    for s, fn in enumerate(sends):
+        due.setdefault(LAG + (3 * s) // 2, []).append(fn)
+    due.setdefault(5, []).append(from_a)
+    due.setdefault(6, []).append(lambda: forward(f, to_b))
+
+    def first_z():
+        from_z(0, 0)
+
+        @pl.when(mid)
+        def _():
+            from_z(1, 0)
+
+    due.setdefault(9, []).append(first_z)
+    due.setdefault(10, []).append(lambda: forward(z * 4 + low_a, to_b))
+    last = max(max(due), len(steps) - 1)
+    for m in range(last + 1):
+        if m < len(steps):
+            steps[m]()
+        for fn in due.get(m, []):
+            fn()
+
+    def rest(ends):
+        along(0, 1) if ends else None
+        partial(low, 0)
+        along(0, 0) if ends else None
+        partial(low, 1)
+        from_z(0, 1)
+        if not ends:
+            from_z(1, 1)
+        partial(low, 2)
+        along(1, 1) if ends else None
+        partial(low, 3)
+        use(f, True)
+        from_b(z, 0)
+        if ends:
+            from_z(1, 0)
+            use_when(close(0), low)
+            along(1, 0)
+            from_b(z, 1)
+            use_when(z, low_b)
+            from_z(1, 1)
+            along(2, 1)
+            use_when(close(1), low)
+            from_b(close(0), 0)
+            from_z(2, 0)
+            along(2, 0)
+            use_when(z, low_a)
+            from_b(close(0), 1)
+            use_when(z, low_ab)
+            from_z(2, 1)
+            from_b(close(1), 0)
+        else:
+            from_z(2, 0)
+            along(0, 1)
+            use_when(close(0), low)
+            use_when(close(1), low)
+            from_b(z, 1)
+            from_z(2, 1)
+            along(0, 0)
+            use_when(z, low_b)
+            along(3, 1)
+            from_b(close(0), 0)
+            use_when(z, low_a)
+            along(1, 1)
+            use_when(z, low_ab)
+            from_b(close(1), 0)
+            along(3, 0)
+            along(1, 0)
+            from_b(close(0), 1)
+
+    @pl.when(mid)
+    def _():
+        rest(False)
+
+    @pl.when(jnp.logical_not(mid))
+    def _():
+        rest(True)
+
+    use_when(close(2), low)
+    use_when(close(0), low_b)
+    use_when(close(0), low_a)
+    t3[...] = settle(1).astype(BF16)
+    send(t3, r3, r3_recv, to_a)
+    from_b(close(1), 1)
+    use_when(close(1), low_b)
+    use_when(close(1), low_a)
+    use_when(close(0), low_ab)
+    total = settle(0)
+    arrived(r3, r3_recv)
+    fin[d] = total + r3[...].astype(F32)
+    for s in range(1, dp):
+        send(fin.at[d], fin.at[d], fin_recv.at[d], dev(f, lax.rem(d + s, dp)))
+    from_b(close(2), 0)
+    use_when(close(1), low_ab)
+    use_when(close(2), low_b)
+    from_b(close(2), 1)
+    use_when(close(2), low_a)
+    loads[-1].wait()
+    for s in range(1, dp):
+        src = lax.rem(d + s, dp)
+        arrived(fin.at[src], fin_recv.at[src])
+    for h in range(2):
+        total = fin[h]
+        for g in range(1, dp // 2):
+            total = total + fin[2 * g + h]
+        side = slice(h * half, (h + 1) * half)
+        gb[:, side] = main[:, side] + total * scale
+    use_when(close(2), low_ab)
+    key[...] = acc[...].astype(BF16)
+
+    per_z = jnp.where(has_up, z + 1, 0) + jnp.where(has_dn, depth - z, 0)
+    blocks = 4 + 6 * (depth - 1) + 8 * depth + 1 + 2 * per_z
+
+    def left(_, carry):
+        send_done(give.at[f])
+        return carry
+
+    def send_done(src):
+        pltpu.make_async_remote_copy(
+            src_ref=src, dst_ref=src, send_sem=send_sem, recv_sem=r3_recv, device_id=to_sib, device_id_type=MESH
+        ).wait_send()
+
+    lax.fori_loop(0, blocks, left, 0)
+    for s in range(1, dp):
+        send_done(fin.at[d])
+
+
+def place(order, key, ig, gb, key_hbm, ig_hbm, gb_hbm, sem):
+    n, _, chunk = ig.shape
+    puts = []
+    for fb in range(n):
+        there = pl.ds(pl.multiple_of(order[fb] * chunk, chunk), chunk)
+        puts.append(pltpu.make_async_copy(ig.at[fb], ig_hbm.at[:, there], sem.at[fb]))
+    puts.append(pltpu.make_async_copy(key, key_hbm, sem.at[n]))
+    puts.append(pltpu.make_async_copy(gb, gb_hbm, sem.at[n + 1]))
+    for cp in puts:
+        cp.start()
+    for cp in puts:
+        cp.wait()
+
+
+def near(x, c, w, main, order, n, dp, scale):
+    rows, width = x.shape
+    chunk, key_width = main.shape
+    half = key_width // 2
+    depth = n // 4
+    dma = pltpu.SemaphoreType.DMA
+    block = (chunk, half)
+    hbm = pl.BlockSpec(memory_space=pltpu.HBM)
+    smem = pl.BlockSpec(memory_space=pltpu.SMEM)
+    vmem = pl.BlockSpec(memory_space=pltpu.VMEM)
+    operands = [pltpu.with_memory_space_constraint(a, pltpu.HBM) for a in (order, x, c, w, main)]
+    key, ig, gb, order = pl.pallas_call(
+        functools.partial(exchange, n, dp, scale),
+        out_shape=(
+            pltpu.VMEM((rows, key_width), BF16),
+            pltpu.VMEM((n, rows, chunk), BF16),
+            pltpu.VMEM((chunk, key_width), F32),
+            pltpu.SMEM((n,), jnp.int32),
+        ),
+        in_specs=[hbm] * 5,
+        out_specs=(vmem,) * 3 + (smem,),
+        scratch_shapes=[
+            pltpu.VMEM((n, rows, chunk), BF16),
+            pltpu.VMEM((rows, key_width), BF16),
+            pltpu.VMEM((rows, key_width), BF16),
+            pltpu.VMEM((2, n) + block, BF16),
+            pltpu.VMEM((n,) + block, F32),
+            pltpu.VMEM((n,) + block, BF16),
+            pltpu.VMEM((n,) + block, BF16),
+            pltpu.VMEM((n,) + block, BF16),
+            pltpu.VMEM((2, depth) + block, BF16),
+            pltpu.VMEM((2, depth) + block, BF16),
+            pltpu.VMEM((2, depth, 2) + block, BF16),
+            pltpu.VMEM(block, BF16),
+            pltpu.VMEM(block, BF16),
+            pltpu.VMEM((dp,) + block, F32),
+            pltpu.VMEM((chunk, key_width), F32),
+            pltpu.VMEM((rows, key_width), F32),
+            dma((n + 5,)),
+            dma,
+            dma((n,)),
+            dma((n,)),
+            dma((n,)),
+            dma((2, depth)),
+            dma((2, depth, 2)),
+            dma,
+            dma((dp,)),
+        ],
+        compiler_params=pltpu.CompilerParams(
+            collective_id=0, has_side_effects=True, vmem_limit_bytes=36 * 1024 * 1024
+        ),
+    )(*operands)
+    return pl.pallas_call(
+        place,
+        out_shape=(
+            jax.ShapeDtypeStruct((rows, key_width), BF16),
+            jax.ShapeDtypeStruct((rows, width), BF16),
+            jax.ShapeDtypeStruct((chunk, key_width), F32),
+        ),
+        in_specs=[smem] + [vmem] * 3,
+        out_specs=(hbm,) * 3,
+        scratch_shapes=[dma((n + 2,))],
+        compiler_params=pltpu.CompilerParams(vmem_limit_bytes=8 * 1024 * 1024),
+    )(order, key, ig, gb)
+
+
 def body(normed, kv_cotangent, kv_weight, main_grad, owner_order):
     micro_count, tok_dev, width = normed.shape
     shard_rows, key_width = kv_weight.shape
@@ -304,6 +753,15 @@
     depth = n // 4
     scale = 1.0 / math.sqrt(rows * n * dp)
     chunk = shard_rows if shard_rows % 128 == 0 else max(shard_rows, 256)
+    if depth == 4 and shard_rows % 128 == 0:
+        key, ig, gb = near(
+            normed.reshape(rows, width), kv_cotangent.reshape(rows, key_width), kv_weight, main_grad, owner_order, n, dp, scale
+        )
+        return (
+            key.reshape(micro_count, tok_dev, key_width),
+            ig.reshape(micro_count, tok_dev, width),
+            gb,
+        )
     x = reorder(normed.reshape(rows, width), owner_order, False)
     chunks = width // chunk
     dma = pltpu.SemaphoreType.DMA

time: 63.8 us -> 40.5 us (0.63)
  Pallas kernels: 61.4 us -> 39.7 us
  local copies, waits for them, and re-layouts: 1.5 us -> 0 us
    pallas_call x3 -> x2, Pallas kernels: 61.4 us -> 39.7 us  [the longest x1 38 us: near(): pl.pallas_call(functools.partial(exchange, n, dp, scale), out_shape=(pltp...]
    unnamed x6 -> x0, local copies, waits for them, and re-layouts: 1.5 us -> none
where the time goes in v1:
time: 40.5 us; the launch traced here: 40.3 us
  Pallas kernels  39.7 us (98%)
  between operations  0.64 us (2%)
    pallas_call x1, Pallas kernels, near(): pl.pallas_call(functools.partial(exchange, n, dp, scale), out_shape=(pltp...  38 us
    pallas_call x1, Pallas kernels, near(): pl.pallas_call(place, out_shape=(jax.ShapeDtypeStruct((rows, key_width),...  1.73 us

profile of v1, /device:TPU:1, one launch (start us, length us, event | category | flops | bytes accessed | tf_op | source)
XLA Modules:
  0.0 40.3 jit_solution(1203230645916817549)
XLA Ops:
  0.6 38.0 %shard_map.76 = (bf16[256,512]{1,0:T(8,128)(2,1)S(1)}, bf16[16,256,256]{2,1,0:T(8,128)(2,1)S(1)}, f32[256,512]{1,0:T(8,128)S(1)}, s32[16]{0:T(128)S(4)}) custom-call(s32[16]{0:T(128)} %order_hbm.1, bf16[256,4096]{1,0:T(8,128)(2,1)} %bitcast.4, bf16[256,512]{1,0:T(8,128)(2,1)} %bitcast.5, bf16[256,512]{1,0:T(8,128)(2,1)} %w_hbm.1, f32[256,512]{1,0:T(8,128)} %main_hbm.1), custom_call_target="tpu_custom_call" | custom-call | tf_op jit(solution)/shard_map/pallas_call | solution.py:691
  38.6 1.7 %shard_map.77 = (bf16[256,512]{1,0:T(8,128)(2,1)}, bf16[256,4096]{1,0:T(8,128)(2,1)}, f32[256,512]{1,0:T(8,128)}) custom-call(s32[16]{0:T(128)S(4)} %get-tuple-element.10.order, bf16[256,512]{1,0:T(8,128)(2,1)S(1)} %get-tuple-element.11.key, bf16[16,256,256]{2,1,0:T(8,128)(2,1)S(1)} %get-tuple-element.12.ig, f32[256,512]{1,0:T(8,128)S(1)} %get-tuple-element.13.gb), custom_call_target="tpu_custom_call" | custom-call | tf_op jit(solution)/shard_map/pallas_call | solution.py:732

commit v2 on v1

--- a/solution.py
+++ b/solution.py
@@ -322,13 +322,13 @@
     has_dn = z > 0
     mid = jnp.logical_and(has_up, has_dn)
 
-    def far(t):
-        return (1 - upper) * (depth - 1 - t) + upper * t
-
     def close(i):
         up = i + jnp.where(i >= z, 1, 0)
         dn = depth - 1 - i - jnp.where(depth - 1 - i <= z, 1, 0)
         return (1 - upper) * up + upper * dn
+
+    def far(t):
+        return close(depth - 2 - t) if t < depth - 1 else z
 
     def dev(fi, di):
         return {"fsdp": fi, "dp": di}
@@ -455,19 +455,16 @@
 
     def along(t, j):
         zz = far(t)
-
-        @pl.when(zz != z)
+        side = jnp.where(zz > z, 0, 1)
+        edge = jnp.where(zz > z, z == 0, z == depth - 1)
+
+        @pl.when(jnp.logical_not(edge))
         def _():
-            side = jnp.where(zz > z, 0, 1)
-            edge = jnp.where(zz > z, z == 0, z == depth - 1)
-
-            @pl.when(jnp.logical_not(edge))
-            def _():
-                arrived(zin.at[side, zz, j], z_recv.at[side, zz, j])
-
-            total = ready(j, zz) + zin[side, zz, j].astype(F32)
-            hop[j, zz] = total.astype(BF16)
-            send(hop.at[j, zz], zin.at[side, zz, j], z_recv.at[side, zz, j], level(z + 1 - 2 * side))
+            arrived(zin.at[side, zz, j], z_recv.at[side, zz, j])
+
+        total = ready(j, zz) + zin[side, zz, j].astype(F32)
+        hop[j, zz] = total.astype(BF16)
+        send(hop.at[j, zz], zin.at[side, zz, j], z_recv.at[side, zz, j], level(z + 1 - 2 * side))
 
     def settle(j):
         total = ready(j, z)
@@ -524,112 +521,98 @@
     for cp in load_x:
         cp.wait()
 
-    steps = []
-    for t in range(depth):
-        steps += [
-            functools.partial(partial, low_ab, t),
-            functools.partial(partial, low_a, t),
-            functools.partial(partial, low_b, t),
-        ]
-    sends = []
-    for t in range(depth):
-        sends += [functools.partial(across, 1, t), functools.partial(across, 0, t)]
-    LAG = 3
-    due = {}
-    for s, fn in enumerate(sends):
-        due.setdefault(LAG + (3 * s) // 2, []).append(fn)
-    due.setdefault(5, []).append(from_a)
-    due.setdefault(6, []).append(lambda: forward(f, to_b))
-
-    def first_z():
-        from_z(0, 0)
-
-        @pl.when(mid)
-        def _():
-            from_z(1, 0)
-
-    due.setdefault(9, []).append(first_z)
-    due.setdefault(10, []).append(lambda: forward(z * 4 + low_a, to_b))
-    last = max(max(due), len(steps) - 1)
-    for m in range(last + 1):
-        if m < len(steps):
-            steps[m]()
-        for fn in due.get(m, []):
-            fn()
-
-    def rest(ends):
-        along(0, 1) if ends else None
-        partial(low, 0)
-        along(0, 0) if ends else None
-        partial(low, 1)
+    def start(*kinds):
+        for kind, t in kinds:
+            if kind == "p":
+                partial(low_ab, t)
+                partial(low_a, t)
+                partial(low_b, t)
+            else:
+                across(1, t)
+                across(0, t)
+
+    start(("p", 0), ("p", 1), ("s", 0), ("p", 2), ("s", 1))
+    from_a()
+    forward(f, to_b)
+    forward(z * 4 + low_a, to_b)
+    start(("p", 3), ("s", 2))
+    from_z(0, 0)
+
+    @pl.when(mid)
+    def _():
+        from_z(1, 0)
+
+    across(1, 3)
+    across(0, 3)
+    partial(low, 0)
+    partial(low, 1)
+
+    @pl.when(jnp.logical_not(mid))
+    def _():
+        along(0, 1)
+        along(0, 0)
+        partial(low, 2)
         from_z(0, 1)
-        if not ends:
-            from_z(1, 1)
-        partial(low, 2)
-        along(1, 1) if ends else None
+        along(1, 1)
         partial(low, 3)
         use(f, True)
         from_b(z, 0)
-        if ends:
-            from_z(1, 0)
-            use_when(close(0), low)
-            along(1, 0)
-            from_b(z, 1)
-            use_when(z, low_b)
-            from_z(1, 1)
-            along(2, 1)
-            use_when(close(1), low)
-            from_b(close(0), 0)
-            from_z(2, 0)
-            along(2, 0)
-            use_when(z, low_a)
-            from_b(close(0), 1)
-            use_when(z, low_ab)
-            from_z(2, 1)
-            from_b(close(1), 0)
-        else:
-            from_z(2, 0)
-            along(0, 1)
-            use_when(close(0), low)
-            use_when(close(1), low)
-            from_b(z, 1)
-            from_z(2, 1)
-            along(0, 0)
-            use_when(z, low_b)
-            along(3, 1)
-            from_b(close(0), 0)
-            use_when(z, low_a)
-            along(1, 1)
-            use_when(z, low_ab)
-            from_b(close(1), 0)
-            along(3, 0)
-            along(1, 0)
-            from_b(close(0), 1)
+        from_z(1, 0)
+        along(1, 0)
+        use_when(close(0), low)
+        from_z(1, 1)
+        along(2, 1)
+        use_when(close(1), low)
+        from_b(z, 1)
+        along(2, 0)
+        use_when(z, low_b)
+        use_when(z, low_a)
+        from_z(2, 0)
+        from_b(close(0), 0)
+        from_z(2, 1)
 
     @pl.when(mid)
     def _():
-        rest(False)
-
-    @pl.when(jnp.logical_not(mid))
-    def _():
-        rest(True)
+        partial(low, 2)
+        from_z(0, 1)
+        from_z(1, 1)
+        partial(low, 3)
+        use(f, True)
+        from_b(z, 0)
+        from_z(2, 0)
+        along(0, 1)
+        use_when(close(0), low)
+        use_when(close(1), low)
+        from_z(2, 1)
+        along(0, 0)
+        use_when(z, low_b)
+        along(2, 1)
+        from_b(z, 1)
+        along(1, 1)
+        use_when(z, low_a)
+        along(2, 0)
+        from_b(close(0), 0)
+        along(1, 0)
 
     use_when(close(2), low)
+    use_when(z, low_ab)
+    t3[...] = settle(1).astype(BF16)
+    send(t3, r3, r3_recv, to_a)
+    from_b(close(0), 1)
     use_when(close(0), low_b)
     use_when(close(0), low_a)
-    t3[...] = settle(1).astype(BF16)
-    send(t3, r3, r3_recv, to_a)
+    from_b(close(1), 0)
+    use_when(close(0), low_ab)
+    use_when(close(1), low_b)
+    total = settle(0)
     from_b(close(1), 1)
-    use_when(close(1), low_b)
     use_when(close(1), low_a)
-    use_when(close(0), low_ab)
-    total = settle(0)
     arrived(r3, r3_recv)
     fin[d] = total + r3[...].astype(F32)
     for s in range(1, dp):
         send(fin.at[d], fin.at[d], fin_recv.at[d], dev(f, lax.rem(d + s, dp)))
+    use_when(close(1), low_ab)
     from_b(close(2), 0)
-    use_when(close(1), low_ab)
     use_when(close(2), low_b)
     from_b(close(2), 1)
     use_when(close(2), low_a)

time: 40.5 us -> 37.3 us (0.921)
  Pallas kernels: 39.7 us -> 36.5 us
    pallas_call x1, Pallas kernels: 38 us -> 34.8 us  [near(): pl.pallas_call(functools.partial(exchange, n, dp, scale), out_shape=(pltp...]
where the time goes in v2:
time: 37.3 us; the launch traced here: 37.1 us
  Pallas kernels  36.5 us (98%)
  between operations  0.64 us (2%)
    pallas_call x1, Pallas kernels, near(): pl.pallas_call(functools.partial(exchange, n, dp, scale), out_shape=(pltp...  34.8 us
    pallas_call x1, Pallas kernels, near(): pl.pallas_call(place, out_shape=(jax.ShapeDtypeStruct((rows, key_width),...  1.73 us

profile of v2, /device:TPU:1, one launch (start us, length us, event | category | flops | bytes accessed | tf_op | source)
XLA Modules:
  0.0 37.1 jit_solution(1374594938572660192)
XLA Ops:
  0.6 34.8 %shard_map.76 = (bf16[256,512]{1,0:T(8,128)(2,1)S(1)}, bf16[16,256,256]{2,1,0:T(8,128)(2,1)S(1)}, f32[256,512]{1,0:T(8,128)S(1)}, s32[16]{0:T(128)S(4)}) custom-call(s32[16]{0:T(128)} %order_hbm.1, bf16[256,4096]{1,0:T(8,128)(2,1)} %bitcast.4, bf16[256,512]{1,0:T(8,128)(2,1)} %bitcast.5, bf16[256,512]{1,0:T(8,128)(2,1)} %w_hbm.1, f32[256,512]{1,0:T(8,128)} %main_hbm.1), custom_call_target="tpu_custom_call" | custom-call | tf_op jit(solution)/shard_map/pallas_call | solution.py:674
  35.4 1.7 %shard_map.77 = (bf16[256,512]{1,0:T(8,128)(2,1)}, bf16[256,4096]{1,0:T(8,128)(2,1)}, f32[256,512]{1,0:T(8,128)}) custom-call(s32[16]{0:T(128)S(4)} %get-tuple-element.10.order, bf16[256,512]{1,0:T(8,128)(2,1)S(1)} %get-tuple-element.11.key, bf16[16,256,256]{2,1,0:T(8,128)(2,1)S(1)} %get-tuple-element.12.ig, f32[256,512]{1,0:T(8,128)S(1)} %get-tuple-element.13.gb), custom_call_target="tpu_custom_call" | custom-call | tf_op jit(solution)/shard_map/pallas_call | solution.py:715

commit v3 on v2

--- a/solution.py
+++ b/solution.py
@@ -11,6 +11,8 @@
 MESH = pl.DeviceIdType.MESH
 F32 = jnp.float32
 BF16 = jnp.bfloat16
+SLOT = (0, 1, 1, 2)
+SWAP = (0, 2, 1, 3)
 
 
 def kernel(
@@ -299,7 +301,7 @@
     order_hbm, x_hbm, c_hbm, w_hbm, main_hbm,
     key, ig, gb, order,
     xx, cc, ck, gath, mine, give, take, part, r1, hop, zin, t3, r3, fin, main, acc,
-    load_sem, send_sem, ag_recv, sib_recv, take_recv, r1_recv, z_recv, r3_recv, fin_recv,
+    load_sem, send_sem, ag_recv, b_recv, sib_recv, take_recv, r1_recv, z_recv, r3_recv, fin_recv,
 ):
     f = lax.axis_index("fsdp")
     d = lax.axis_index("dp")
@@ -307,6 +309,7 @@
     sib = d + 1 - 2 * k
     chunk, key_width = main_hbm.shape
     half = key_width // 2
+    part_rows = chunk // 2
     depth = n // 4
     z = lax.div(f, 4)
     low = lax.rem(f, 4)
@@ -317,6 +320,7 @@
     low_a = flip0 + k * (flip1 - flip0)
     low_b = flip1 + k * (flip0 - flip1)
     low_ab = 3 - low
+    lows = (low, low_a, low_b, low_ab)
     upper = lax.div(2 * z, depth)
     has_up = z < depth - 1
     has_dn = z > 0
@@ -347,14 +351,17 @@
         cp.start()
         loads.append(cp)
 
-    load(w_hbm.at[:, pl.ds(0, half)], gath.at[0, f])
-    load(w_hbm.at[:, pl.ds(half, half)], gath.at[1, f])
+    def loaded(*span):
+        for cp in loads[slice(*span)]:
+            cp.wait()
+
+    load(w_hbm.at[:, pl.ds(0, half)], gath.at[0, z, 0])
+    load(w_hbm.at[:, pl.ds(half, half)], gath.at[1, z, 0])
     load(order_hbm, order)
     load(c_hbm, cc)
     for j in range(n):
         load(x_hbm.at[:, pl.ds(j * chunk, chunk)], xx.at[j])
     load(main_hbm, main)
-    load_x = loads[4 : 4 + n]
 
     barrier = pltpu.get_barrier_semaphore()
 
@@ -396,92 +403,112 @@
             src_ref=dst, dst_ref=dst, send_sem=send_sem, recv_sem=rsem, device_id=to_sib, device_id_type=MESH
         ).wait_recv()
 
-    def block(fb):
-        return gath.at[k, fb]
-
-    def forward(fb, to, cond=None):
-        send(block(fb), block(fb), ag_recv.at[fb], to, cond)
-
-    def forward_sib(fb):
-        send(block(fb), block(fb), sib_recv.at[fb], to_sib)
+    def rows_of(p):
+        return pl.ds(p * part_rows, part_rows)
+
+    def forward(zz, kind):
+        send(gath.at[k, zz, kind], gath.at[k, zz, kind + 2], b_recv.at[kind, zz], to_b)
+
+    def forward_piece(zz, kind, there, p, to, cond=None):
+        src = gath.at[k, zz, kind, rows_of(p)]
+        dst = gath.at[k, zz, there, rows_of(p)]
+        send(src, dst, ag_recv.at[there, zz, p], to, cond)
+
+    def forward_sib(zz, kind):
+        send(gath.at[k, zz, kind], gath.at[k, zz, SWAP[kind]], sib_recv.at[SLOT[kind], zz], to_sib)
 
     contract_rows = (((0,), (0,)), ((), ()))
     contract_cols = (((1,), (1,)), ((), ()))
 
-    def partial(lo, t):
-        fb = far(t) * 4 + lo
-        prod = lax.dot_general(xx[order[fb]], ck[...], contract_rows, preferred_element_type=F32)
-        give[fb] = prod[:, half:].astype(BF16)
-        send(give.at[fb], take.at[fb], take_recv.at[fb], to_sib)
-        mine[fb] = prod[:, :half]
-
-    def pair(fb):
-        return mine[fb] + take[fb].astype(F32)
+    def partial(kind, t):
+        zz = far(t)
+        prod = lax.dot_general(xx[order[zz * 4 + lows[kind]]], ck[...], contract_rows, preferred_element_type=F32)
+        give[zz, kind] = prod[:, half:].astype(BF16)
+        there = 3 - SWAP[kind]
+        send(give.at[zz, kind], take.at[zz, there], take_recv.at[there // 2, zz], to_sib)
+        mine[zz, kind] = prod[:, :half]
+
+    def taken(group, zz):
+        arrived(take.at[zz, pl.ds(2 * group, 2)], take_recv.at[group, zz])
+
+    def pair(zz, kind, span):
+        return mine[zz, kind, span] + take[zz, 3 - kind, span].astype(F32)
 
     def across(j, t):
         zz = far(t)
-        fb = zz * 4 + (low_ab if j else low_b)
-        arrived(take.at[fb], take_recv.at[fb])
-        part[fb] = pair(fb).astype(BF16)
-        send(part.at[fb], r1.at[j, zz], r1_recv.at[j, zz], to_b)
-
-    def from_a():
-        fb = z * 4 + low_a
-        arrived(block(fb), ag_recv.at[fb])
-        forward(fb, level(z + 1), has_up)
-        forward(fb, level(z - 1), has_dn)
-        forward_sib(fb)
-
-    def from_z(i, j):
+        if j:
+            taken(0, zz)
+        part[j, zz] = pair(zz, 2 + j, slice(None)).astype(BF16)
+        send(part.at[j, zz], r1.at[j, zz], r1_recv.at[j, zz], to_b)
+
+    def from_a(p):
+        arrived(gath.at[k, z, 1, rows_of(p)], ag_recv.at[1, z, p])
+        forward_piece(z, 1, 1, p, level(z + 1), has_up)
+        forward_piece(z, 1, 1, p, level(z - 1), has_dn)
+        if p:
+            forward(z, 1)
+            forward_sib(z, 1)
+
+    def from_z(i, j, p):
         zz = close(i)
-        fb = zz * 4 + (low_a if j else low)
-        arrived(block(fb), ag_recv.at[fb])
+        arrived(gath.at[k, zz, j, rows_of(p)], ag_recv.at[j, zz, p])
         below = zz < z
         on = jnp.logical_or(jnp.logical_and(below, has_up), jnp.logical_and(zz > z, has_dn))
-        forward(fb, level(z + jnp.where(below, 1, -1)), on)
-        forward(fb, to_b)
-        forward_sib(fb)
+        forward_piece(zz, j, j, p, level(z + jnp.where(below, 1, -1)), on)
+        if p:
+            forward(zz, j)
+            forward_sib(zz, j)
 
     def from_b(zz, j):
-        fb = zz * 4 + (low_ab if j else low_b)
-        arrived(block(fb), ag_recv.at[fb])
-        forward_sib(fb)
+        arrived(gath.at[k, zz, 2 + j], b_recv.at[j, zz])
+        forward_sib(zz, 2 + j)
 
     def ready(j, zz):
-        fb = zz * 4 + (low_a if j else low)
-        arrived(take.at[fb], take_recv.at[fb])
+        if j:
+            taken(1, zz)
         arrived(r1.at[j, zz], r1_recv.at[j, zz])
-        return pair(fb) + r1[j, zz].astype(F32)
-
-    def along(t, j):
+
+    def summed(j, zz, span):
+        return pair(zz, j, span) + r1[j, zz, span].astype(F32)
+
+    def along(t, j, p):
         zz = far(t)
         side = jnp.where(zz > z, 0, 1)
         edge = jnp.where(zz > z, z == 0, z == depth - 1)
+        span = rows_of(p)
+        spot = zin.at[side, zz, j, span]
+        if not p:
+            ready(j, zz)
 
         @pl.when(jnp.logical_not(edge))
         def _():
-            arrived(zin.at[side, zz, j], z_recv.at[side, zz, j])
-
-        total = ready(j, zz) + zin[side, zz, j].astype(F32)
-        hop[j, zz] = total.astype(BF16)
-        send(hop.at[j, zz], zin.at[side, zz, j], z_recv.at[side, zz, j], level(z + 1 - 2 * side))
-
-    def settle(j):
-        total = ready(j, z)
+            arrived(spot, z_recv.at[zz, j, p])
+
+        total = summed(j, zz, span) + spot[...].astype(F32)
+        hop[j, zz, span] = total.astype(BF16)
+        there = z + 1 - 2 * side
+        slot = jnp.where(side * depth + zz == depth + there, depth, zz)
+        send(hop.at[j, zz, span], spot, z_recv.at[slot, j, p], level(there))
+
+    def settle(j, p):
+        span = rows_of(p)
+        if not p:
+            ready(j, z)
 
         @pl.when(has_dn)
         def _():
-            arrived(zin.at[0, z, j], z_recv.at[0, z, j])
+            arrived(zin.at[0, z, j, span], z_recv.at[z, j, p])
 
         @pl.when(has_up)
         def _():
-            arrived(zin.at[1, z, j], z_recv.at[1, z, j])
-
-        return total + zin[0, z, j].astype(F32) + zin[1, z, j].astype(F32)
-
-    def use(fb, first=False):
-        w0 = gath[0, fb]
-        w1 = gath[1, fb]
+            arrived(zin.at[1, z, j, span], z_recv.at[depth, j, p])
+
+        return summed(j, z, span) + zin[0, z, j, span].astype(F32) + zin[1, z, j, span].astype(F32)
+
+    def use(zz, kind, first=False):
+        fb = zz * 4 + lows[kind]
+        w0 = gath[0, zz, kind]
+        w1 = gath[1, zz, kind]
         prod = lax.dot_general(cc[:, :half], w0, contract_cols, preferred_element_type=F32)
         prod = prod + lax.dot_general(cc[:, half:], w1, contract_cols, preferred_element_type=F32)
         ig[fb] = prod.astype(BF16)
@@ -495,16 +522,16 @@
             acc[:, :half] += k0
             acc[:, half:] += k1
 
-    def use_when(zz, lo):
-        fb = zz * 4 + lo
-        arrived(gath.at[1 - k, fb], sib_recv.at[fb])
-        use(fb)
-
-    loads[0].wait()
-    loads[1].wait()
-    forward(f, to_a)
-    forward(f, level(z + 1), has_up)
-    forward(f, level(z - 1), has_dn)
+    def use_when(zz, *kinds):
+        arrived(gath.at[1 - k, zz, pl.ds(kinds[0], len(kinds))], sib_recv.at[SLOT[kinds[0]], zz])
+        for kind in kinds:
+            use(zz, kind)
+
+    loaded(0, 2)
+    for p in range(2):
+        forward_piece(z, 0, 1, p, to_a)
+        forward_piece(z, 0, 0, p, level(z + 1), has_up)
+        forward_piece(z, 0, 0, p, level(z - 1), has_dn)
 
     @pl.when(z == 0)
     def _():
@@ -514,109 +541,117 @@
     def _():
         zin[1] = jnp.zeros(zin.shape[1:], BF16)
 
-    loads[3].wait()
+    loaded(2, -1)
     ck[:, :half] = cc[:, pl.ds(pl.multiple_of(k * half, half), half)]
     ck[:, half:] = cc[:, pl.ds(pl.multiple_of((1 - k) * half, half), half)]
-    loads[2].wait()
-    for cp in load_x:
-        cp.wait()
-
-    def start(*kinds):
-        for kind, t in kinds:
-            if kind == "p":
-                partial(low_ab, t)
-                partial(low_a, t)
-                partial(low_b, t)
+    def start(*tasks):
+        for what, t in tasks:
+            if what == "p":
+                partial(3, t)
+                partial(1, t)
+                partial(2, t)
             else:
                 across(1, t)
                 across(0, t)
 
-    start(("p", 0), ("p", 1), ("s", 0), ("p", 2), ("s", 1))
-    from_a()
-    forward(f, to_b)
-    forward(z * 4 + low_a, to_b)
+    start(("p", 0))
+    partial(3, 1)
+    forward(z, 0)
+    partial(1, 1)
+    partial(2, 1)
+    start(("s", 0), ("p", 2))
+    from_a(0)
+    start(("s", 1))
+    from_a(1)
     start(("p", 3), ("s", 2))
-    from_z(0, 0)
+    for p in range(2):
+        from_z(0, 0, p)
+
+        @pl.when(mid)
+        def _():
+            from_z(1, 0, p)
+
+    start(("s", 3))
+    partial(0, 0)
+    partial(0, 1)
+
+    def both(fn, *args):
+        fn(*args, 0)
+        fn(*args, 1)
+
+    @pl.when(jnp.logical_not(mid))
+    def _():
+        both(along, 0, 1)
+        partial(0, 2)
+        both(along, 0, 0)
+        both(from_z, 0, 1)
+        both(along, 1, 1)
+        partial(0, 3)
+        use(z, 0, True)
+        both(along, 1, 0)
+        both(from_z, 1, 0)
+        from_b(z, 0)
+        use_when(close(0), 0)
+        from_z(1, 1, 0)
+        both(along, 2, 1)
+        from_z(1, 1, 1)
+        both(along, 2, 0)
+        use_when(close(1), 0)
+        both(from_z, 2, 0)
+        from_b(z, 1)
+        use_when(z, 1, 2)
+        from_b(close(0), 0)
+        both(from_z, 2, 1)
 
     @pl.when(mid)
     def _():
-        from_z(1, 0)
-
-    across(1, 3)
-    across(0, 3)
-    partial(low, 0)
-    partial(low, 1)
-
-    @pl.when(jnp.logical_not(mid))
-    def _():
-        along(0, 1)
-        along(0, 0)
-        partial(low, 2)
-        from_z(0, 1)
-        along(1, 1)
-        partial(low, 3)
-        use(f, True)
+        partial(0, 2)
+        from_z(0, 1, 0)
+        from_z(1, 1, 0)
+        from_z(0, 1, 1)
+        from_z(1, 1, 1)
+        partial(0, 3)
+        use(z, 0, True)
+        both(from_z, 2, 0)
+        both(along, 0, 1)
         from_b(z, 0)
-        from_z(1, 0)
-        along(1, 0)
-        use_when(close(0), low)
-        from_z(1, 1)
-        along(2, 1)
-        use_when(close(1), low)
+        use_when(close(0), 0)
+        along(0, 0, 0)
+        from_z(2, 1, 0)
+        along(0, 0, 1)
+        from_z(2, 1, 1)
+        use_when(close(1), 0)
+        both(along, 2, 1)
+        both(along, 1, 1)
         from_b(z, 1)
-        along(2, 0)
-        use_when(z, low_b)
-        use_when(z, low_a)
-        from_z(2, 0)
+        both(along, 2, 0)
+        use_when(z, 1, 2)
         from_b(close(0), 0)
-        from_z(2, 1)
-
-    @pl.when(mid)
-    def _():
-        partial(low, 2)
-        from_z(0, 1)
-        from_z(1, 1)
-        partial(low, 3)
-        use(f, True)
-        from_b(z, 0)
-        from_z(2, 0)
-        along(0, 1)
-        use_when(close(0), low)
-        use_when(close(1), low)
-        from_z(2, 1)
-        along(0, 0)
-        use_when(z, low_b)
-        along(2, 1)
-        from_b(z, 1)
-        along(1, 1)
-        use_when(z, low_a)
-        along(2, 0)
-        from_b(close(0), 0)
-        along(1, 0)
-
-    use_when(close(2), low)
-    use_when(z, low_ab)
-    t3[...] = settle(1).astype(BF16)
-    send(t3, r3, r3_recv, to_a)
+        both(along, 1, 0)
+
+    use_when(close(2), 0)
+    use_when(z, 3)
+    for p in range(2):
+        t3[rows_of(p)] = settle(1, p).astype(BF16)
+        send(t3.at[rows_of(p)], r3.at[rows_of(p)], r3_recv.at[p], to_a)
     from_b(close(0), 1)
-    use_when(close(0), low_b)
-    use_when(close(0), low_a)
+    use_when(close(0), 1, 2)
     from_b(close(1), 0)
-    use_when(close(0), low_ab)
-    use_when(close(1), low_b)
-    total = settle(0)
+    use_when(close(0), 3)
     from_b(close(1), 1)
-    use_when(close(1), low_a)
-    arrived(r3, r3_recv)
-    fin[d] = total + r3[...].astype(F32)
+    use_when(close(1), 1, 2)
+    from_b(close(2), 0)
+    use_when(close(1), 3)
+    for p in range(2):
+        fin[d, rows_of(p)] = settle(0, p)
+    for p in range(2):
+        arrived(r3.at[rows_of(p)], r3_recv.at[p])
+        fin[d, rows_of(p)] += r3[rows_of(p)].astype(F32)
     for s in range(1, dp):
         send(fin.at[d], fin.at[d], fin_recv.at[d], dev(f, lax.rem(d + s, dp)))
-    use_when(close(1), low_ab)
-    from_b(close(2), 0)
-    use_when(close(2), low_b)
     from_b(close(2), 1)
-    use_when(close(2), low_a)
-    loads[-1].wait()
+    use_when(close(2), 1, 2)
+    loaded(-1, None)
     for s in range(1, dp):
         src = lax.rem(d + s, dp)
         arrived(fin.at[src], fin_recv.at[src])
@@ -626,22 +661,23 @@
             total = total + fin[2 * g + h]
         side = slice(h * half, (h + 1) * half)
         gb[:, side] = main[:, side] + total * scale
-    use_when(close(2), low_ab)
+    use_when(close(2), 3)
     key[...] = acc[...].astype(BF16)
-
-    per_z = jnp.where(has_up, z + 1, 0) + jnp.where(has_dn, depth - z, 0)
-    blocks = 4 + 6 * (depth - 1) + 8 * depth + 1 + 2 * per_z
-
-    def left(_, carry):
-        send_done(give.at[f])
-        return carry
 
     def send_done(src):
         pltpu.make_async_remote_copy(
-            src_ref=src, dst_ref=src, send_sem=send_sem, recv_sem=r3_recv, device_id=to_sib, device_id_type=MESH
+            src_ref=src, dst_ref=src, send_sem=send_sem, recv_sem=r3_recv.at[0], device_id=to_sib, device_id_type=MESH
         ).wait_send()
 
-    lax.fori_loop(0, blocks, left, 0)
+    def left(_, carry):
+        send_done(give.at[0, 0])
+        return carry
+
+    blocks = 4 + 6 * (depth - 1) + 8 * depth + 1
+    for _ in range(blocks // n):
+        send_done(give)
+    per_z = jnp.where(has_up, z + 1, 0) + jnp.where(has_dn, depth - z, 0)
+    lax.fori_loop(0, blocks % n + 2 * per_z, left, 0)
     for s in range(1, dp):
         send_done(fin.at[d])
 
@@ -685,11 +721,11 @@
             pltpu.VMEM((n, rows, chunk), BF16),
             pltpu.VMEM((rows, key_width), BF16),
             pltpu.VMEM((rows, key_width), BF16),
-            pltpu.VMEM((2, n) + block, BF16),
-            pltpu.VMEM((n,) + block, F32),
-            pltpu.VMEM((n,) + block, BF16),
-            pltpu.VMEM((n,) + block, BF16),
-            pltpu.VMEM((n,) + block, BF16),
+            pltpu.VMEM((2, depth, 4) + block, BF16),
+            pltpu.VMEM((depth, 4) + block, F32),
+            pltpu.VMEM((depth, 4) + block, BF16),
+            pltpu.VMEM((depth, 4) + block, BF16),
+            pltpu.VMEM((2, depth) + block, BF16),
             pltpu.VMEM((2, depth) + block, BF16),
             pltpu.VMEM((2, depth) + block, BF16),
             pltpu.VMEM((2, depth, 2) + block, BF16),
@@ -700,12 +736,13 @@
             pltpu.VMEM((rows, key_width), F32),
             dma((n + 5,)),
             dma,
-            dma((n,)),
-            dma((n,)),
-            dma((n,)),
+            dma((2, depth, 2)),
             dma((2, depth)),
-            dma((2, depth, 2)),
-            dma,
+            dma((3, depth)),
+            dma((2, depth)),
+            dma((2, depth)),
+            dma((depth + 1, 2, 2)),
+            dma((2,)),
             dma((dp,)),
         ],
         compiler_params=pltpu.CompilerParams(

time: 37.3 us -> 36 us (0.965)
  Pallas kernels: 36.5 us -> 35.1 us
    pallas_call x1, Pallas kernels: 34.8 us -> 33.4 us  [near(): pl.pallas_call(functools.partial(exchange, n, dp, scale), out_shape=(pltp...]
where the time goes in v3:
time: 36 us; the launch traced here: 35.8 us
  Pallas kernels  35.1 us (98%)
  between operations  0.64 us (2%)
    pallas_call x1, Pallas kernels, near(): pl.pallas_call(functools.partial(exchange, n, dp, scale), out_shape=(pltp...  33.4 us
    pallas_call x1, Pallas kernels, near(): pl.pallas_call(place, out_shape=(jax.ShapeDtypeStruct((rows, key_width),...  1.73 us

profile of v3, /device:TPU:1, one launch (start us, length us, event | category | flops | bytes accessed | tf_op | source)
XLA Modules:
  0.0 35.8 jit_solution(6288744459692762967)
XLA Ops:
  0.6 33.4 %shard_map.76 = (bf16[256,512]{1,0:T(8,128)(2,1)S(1)}, bf16[16,256,256]{2,1,0:T(8,128)(2,1)S(1)}, f32[256,512]{1,0:T(8,128)S(1)}, s32[16]{0:T(128)S(4)}) custom-call(s32[16]{0:T(128)} %order_hbm.1, bf16[256,4096]{1,0:T(8,128)(2,1)} %bitcast.4, bf16[256,512]{1,0:T(8,128)(2,1)} %bitcast.5, bf16[256,512]{1,0:T(8,128)(2,1)} %w_hbm.1, f32[256,512]{1,0:T(8,128)} %main_hbm.1), custom_call_target="tpu_custom_call" | custom-call | tf_op jit(solution)/shard_map/pallas_call | solution.py:710
  34.1 1.7 %shard_map.77 = (bf16[256,512]{1,0:T(8,128)(2,1)}, bf16[256,4096]{1,0:T(8,128)(2,1)}, f32[256,512]{1,0:T(8,128)}) custom-call(s32[16]{0:T(128)S(4)} %get-tuple-element.10.order, bf16[256,512]{1,0:T(8,128)(2,1)S(1)} %get-tuple-element.11.key, bf16[16,256,256]{2,1,0:T(8,128)(2,1)S(1)} %get-tuple-element.12.ig, f32[256,512]{1,0:T(8,128)S(1)} %get-tuple-element.13.gb), custom_call_target="tpu_custom_call" | custom-call | tf_op jit(solution)/shard_map/pallas_call | solution.py:752

commit v4 on v3

--- a/solution.py
+++ b/solution.py
@@ -344,24 +344,16 @@
     def level(zi):
         return dev(lax.rem(zi + depth, depth) * 4 + low, d)
 
-    loads = []
-
-    def load(src, dst):
-        cp = pltpu.make_async_copy(src, dst, load_sem.at[len(loads)])
-        cp.start()
-        loads.append(cp)
-
-    def loaded(*span):
-        for cp in loads[slice(*span)]:
-            cp.wait()
-
-    load(w_hbm.at[:, pl.ds(0, half)], gath.at[0, z, 0])
-    load(w_hbm.at[:, pl.ds(half, half)], gath.at[1, z, 0])
-    load(order_hbm, order)
-    load(c_hbm, cc)
+    def load(src, dst, i):
+        pltpu.make_async_copy(src, dst, load_sem.at[i]).start()
+
+    load(w_hbm.at[:, pl.ds(0, half)], gath.at[0, z, 0], 0)
+    load(w_hbm.at[:, pl.ds(half, half)], gath.at[1, z, 0], 0)
+    load(order_hbm, order, 1)
+    load(c_hbm, cc, 2)
     for j in range(n):
-        load(x_hbm.at[:, pl.ds(j * chunk, chunk)], xx.at[j])
-    load(main_hbm, main)
+        load(x_hbm.at[:, pl.ds(j * chunk, chunk)], xx.at[j], 3)
+    load(main_hbm, main, 4)
 
     barrier = pltpu.get_barrier_semaphore()
 
@@ -527,7 +519,7 @@
         for kind in kinds:
             use(zz, kind)
 
-    loaded(0, 2)
+    arrived(gath.at[:, z, 0], load_sem.at[0])
     for p in range(2):
         forward_piece(z, 0, 1, p, to_a)
         forward_piece(z, 0, 0, p, level(z + 1), has_up)
@@ -541,7 +533,9 @@
     def _():
         zin[1] = jnp.zeros(zin.shape[1:], BF16)
 
-    loaded(2, -1)
+    pltpu.make_async_copy(order_hbm, order, load_sem.at[1]).wait()
+    pltpu.make_async_copy(c_hbm, cc, load_sem.at[2]).wait()
+    arrived(xx, load_sem.at[3])
     ck[:, :half] = cc[:, pl.ds(pl.multiple_of(k * half, half), half)]
     ck[:, half:] = cc[:, pl.ds(pl.multiple_of((1 - k) * half, half), half)]
     def start(*tasks):
@@ -651,7 +645,7 @@
         send(fin.at[d], fin.at[d], fin_recv.at[d], dev(f, lax.rem(d + s, dp)))
     from_b(close(2), 1)
     use_when(close(2), 1, 2)
-    loaded(-1, None)
+    pltpu.make_async_copy(main_hbm, main, load_sem.at[4]).wait()
     for s in range(1, dp):
         src = lax.rem(d + s, dp)
         arrived(fin.at[src], fin_recv.at[src])
@@ -684,15 +678,14 @@
 
 def place(order, key, ig, gb, key_hbm, ig_hbm, gb_hbm, sem):
     n, _, chunk = ig.shape
-    puts = []
     for fb in range(n):
         there = pl.ds(pl.multiple_of(order[fb] * chunk, chunk), chunk)
-        puts.append(pltpu.make_async_copy(ig.at[fb], ig_hbm.at[:, there], sem.at[fb]))
-    puts.append(pltpu.make_async_copy(key, key_hbm, sem.at[n]))
-    puts.append(pltpu.make_async_copy(gb, gb_hbm, sem.at[n + 1]))
-    for cp in puts:
+        pltpu.make_async_copy(ig.at[fb], ig_hbm.at[:, there], sem.at[0]).start()
+    rest = [pltpu.make_async_copy(gb, gb_hbm, sem.at[1]), pltpu.make_async_copy(key, key_hbm, sem.at[2])]
+    for cp in rest:
         cp.start()
-    for cp in puts:
+    pltpu.make_async_copy(ig_hbm, ig_hbm, sem.at[0]).wait()
+    for cp in rest:
         cp.wait()
 
 
@@ -734,7 +727,7 @@
             pltpu.VMEM((dp,) + block, F32),
             pltpu.VMEM((chunk, key_width), F32),
             pltpu.VMEM((rows, key_width), F32),
-            dma((n + 5,)),
+            dma((5,)),
             dma,
             dma((2, depth, 2)),
             dma((2, depth)),
@@ -758,7 +751,7 @@
         ),
         in_specs=[smem] + [vmem] * 3,
         out_specs=(hbm,) * 3,
-        scratch_shapes=[dma((n + 2,))],
+        scratch_shapes=[dma((3,))],
         compiler_params=pltpu.CompilerParams(vmem_limit_bytes=8 * 1024 * 1024),
     )(order, key, ig, gb)
 

time: 36 us -> 35.7 us (level)
  no operation moved by 1% of the time
where the time goes in v4:
time: 35.7 us; the launch traced here: 35.5 us
  Pallas kernels  34.8 us (97%)
  between operations  0.64 us (2%)
    pallas_call x1, Pallas kernels, near(): pl.pallas_call(functools.partial(exchange, n, dp, scale), out_shape=(pltp...  33.2 us
    pallas_call x1, Pallas kernels, near(): pl.pallas_call(place, out_shape=(jax.ShapeDtypeStruct((rows, key_width),...  1.59 us

profile of v4, /device:TPU:1, one launch (start us, length us, event | category | flops | bytes accessed | tf_op | source)
XLA Modules:
  0.0 35.5 jit_solution(6709797730910119845)
XLA Ops:
  0.6 33.2 %shard_map.76 = (bf16[256,512]{1,0:T(8,128)(2,1)S(1)}, bf16[16,256,256]{2,1,0:T(8,128)(2,1)S(1)}, f32[256,512]{1,0:T(8,128)S(1)}, s32[16]{0:T(128)S(4)}) custom-call(s32[16]{0:T(128)} %order_hbm.1, bf16[256,4096]{1,0:T(8,128)(2,1)} %bitcast.4, bf16[256,512]{1,0:T(8,128)(2,1)} %bitcast.5, bf16[256,512]{1,0:T(8,128)(2,1)} %w_hbm.1, f32[256,512]{1,0:T(8,128)} %main_hbm.1), custom_call_target="tpu_custom_call" | custom-call | tf_op jit(solution)/shard_map/pallas_call | solution.py:703
  33.9 1.6 %shard_map.77 = (bf16[256,512]{1,0:T(8,128)(2,1)}, bf16[256,4096]{1,0:T(8,128)(2,1)}, f32[256,512]{1,0:T(8,128)}) custom-call(s32[16]{0:T(128)S(4)} %get-tuple-element.10.order, bf16[256,512]{1,0:T(8,128)(2,1)S(1)} %get-tuple-element.11.key, bf16[16,256,256]{2,1,0:T(8,128)(2,1)S(1)} %get-tuple-element.12.ig, f32[256,512]{1,0:T(8,128)S(1)} %get-tuple-element.13.gb), custom_call_target="tpu_custom_call" | custom-call | tf_op jit(solution)/shard_map/pallas_call | solution.py:745

commit v5 on v4

--- a/solution.py
+++ b/solution.py
@@ -525,6 +525,8 @@
         forward_piece(z, 0, 0, p, level(z + 1), has_up)
         forward_piece(z, 0, 0, p, level(z - 1), has_dn)
 
+    forward(z, 0)
+
     @pl.when(z == 0)
     def _():
         zin[0] = jnp.zeros(zin.shape[1:], BF16)
@@ -549,11 +551,9 @@
                 across(0, t)
 
     start(("p", 0))
-    partial(3, 1)
-    forward(z, 0)
-    partial(1, 1)
-    partial(2, 1)
-    start(("s", 0), ("p", 2))
+    start(("p", 1), ("s", 0))
+    partial(0, 0)
+    start(("p", 2))
     from_a(0)
     start(("s", 1))
     from_a(1)
@@ -565,17 +565,20 @@
         def _():
             from_z(1, 0, p)
 
-    start(("s", 3))
-    partial(0, 0)
-    partial(0, 1)
-
     def both(fn, *args):
         fn(*args, 0)
         fn(*args, 1)
 
+    partial(0, 1)
+
     @pl.when(jnp.logical_not(mid))
     def _():
         both(along, 0, 1)
+
+    start(("s", 3))
+
+    @pl.when(jnp.logical_not(mid))
+    def _():
         partial(0, 2)
         both(along, 0, 0)
         both(from_z, 0, 1)

time: 35.7 us -> 35.1 us (0.983)
  Pallas kernels: 34.8 us -> 34.3 us
    pallas_call x1, Pallas kernels: 33.2 us -> 32.7 us  [near(): pl.pallas_call(functools.partial(exchange, n, dp, scale), out_shape=(pltp...]
where the time goes in v5:
time: 35.1 us; the launch traced here: 35 us
  Pallas kernels  34.3 us (98%)
  between operations  0.64 us (2%)
    pallas_call x1, Pallas kernels, near(): pl.pallas_call(functools.partial(exchange, n, dp, scale), out_shape=(pltp...  32.7 us
    pallas_call x1, Pallas kernels, near(): pl.pallas_call(place, out_shape=(jax.ShapeDtypeStruct((rows, key_width),...  1.59 us

profile of v5, /device:TPU:1, one launch (start us, length us, event | category | flops | bytes accessed | tf_op | source)
XLA Modules:
  0.0 35.0 jit_solution(10708921896146117248)
XLA Ops:
  0.6 32.7 %shard_map.76 = (bf16[256,512]{1,0:T(8,128)(2,1)S(1)}, bf16[16,256,256]{2,1,0:T(8,128)(2,1)S(1)}, f32[256,512]{1,0:T(8,128)S(1)}, s32[16]{0:T(128)S(4)}) custom-call(s32[16]{0:T(128)} %order_hbm.1, bf16[256,4096]{1,0:T(8,128)(2,1)} %bitcast.4, bf16[256,512]{1,0:T(8,128)(2,1)} %bitcast.5, bf16[256,512]{1,0:T(8,128)(2,1)} %w_hbm.1, f32[256,512]{1,0:T(8,128)} %main_hbm.1), custom_call_target="tpu_custom_call" | custom-call | tf_op jit(solution)/shard_map/pallas_call | solution.py:706
  33.4 1.6 %shard_map.77 = (bf16[256,512]{1,0:T(8,128)(2,1)}, bf16[256,4096]{1,0:T(8,128)(2,1)}, f32[256,512]{1,0:T(8,128)}) custom-call(s32[16]{0:T(128)S(4)} %get-tuple-element.10.order, bf16[256,512]{1,0:T(8,128)(2,1)S(1)} %get-tuple-element.11.key, bf16[16,256,256]{2,1,0:T(8,128)(2,1)S(1)} %get-tuple-element.12.ig, f32[256,512]{1,0:T(8,128)S(1)} %get-tuple-element.13.gb), custom_call_target="tpu_custom_call" | custom-call | tf_op jit(solution)/shard_map/pallas_call | solution.py:748

commit v6 on v5

--- a/solution.py
+++ b/solution.py
@@ -644,14 +644,16 @@
     for p in range(2):
         arrived(r3.at[rows_of(p)], r3_recv.at[p])
         fin[d, rows_of(p)] += r3[rows_of(p)].astype(F32)
-    for s in range(1, dp):
-        send(fin.at[d], fin.at[d], fin_recv.at[d], dev(f, lax.rem(d + s, dp)))
+        own = fin.at[d, rows_of(p)]
+        for s in range(1, dp):
+            send(own, own, fin_recv.at[d, p], dev(f, lax.rem(d + s, dp)))
     from_b(close(2), 1)
     use_when(close(2), 1, 2)
     pltpu.make_async_copy(main_hbm, main, load_sem.at[4]).wait()
     for s in range(1, dp):
         src = lax.rem(d + s, dp)
-        arrived(fin.at[src], fin_recv.at[src])
+        for p in range(2):
+            arrived(fin.at[src, rows_of(p)], fin_recv.at[src, p])
     for h in range(2):
         total = fin[h]
         for g in range(1, dp // 2):
@@ -739,7 +741,7 @@
             dma((2, depth)),
             dma((depth + 1, 2, 2)),
             dma((2,)),
-            dma((dp,)),
+            dma((dp, 2)),
         ],
         compiler_params=pltpu.CompilerParams(
             collective_id=0, has_side_effects=True, vmem_limit_bytes=36 * 1024 * 1024

time: 35.1 us -> 34.9 us (level)
  no operation moved by 1% of the time
where the time goes in v6:
time: 34.9 us; the launch traced here: 34.8 us
  Pallas kernels  34.2 us (98%)
  between operations  0.64 us (2%)
    pallas_call x1, Pallas kernels, near(): pl.pallas_call(functools.partial(exchange, n, dp, scale), out_shape=(pltp...  32.6 us
    pallas_call x1, Pallas kernels, near(): pl.pallas_call(place, out_shape=(jax.ShapeDtypeStruct((rows, key_width),...  1.59 us

profile of v6, /device:TPU:1, one launch (start us, length us, event | category | flops | bytes accessed | tf_op | source)
XLA Modules:
  0.0 34.8 jit_solution(8859698243418303968)
XLA Ops:
  0.6 32.6 %shard_map.76 = (bf16[256,512]{1,0:T(8,128)(2,1)S(1)}, bf16[16,256,256]{2,1,0:T(8,128)(2,1)S(1)}, f32[256,512]{1,0:T(8,128)S(1)}, s32[16]{0:T(128)S(4)}) custom-call(s32[16]{0:T(128)} %order_hbm.1, bf16[256,4096]{1,0:T(8,128)(2,1)} %bitcast.4, bf16[256,512]{1,0:T(8,128)(2,1)} %bitcast.5, bf16[256,512]{1,0:T(8,128)(2,1)} %w_hbm.1, f32[256,512]{1,0:T(8,128)} %main_hbm.1), custom_call_target="tpu_custom_call" | custom-call | tf_op jit(solution)/shard_map/pallas_call | solution.py:708
  33.2 1.6 %shard_map.77 = (bf16[256,512]{1,0:T(8,128)(2,1)}, bf16[256,4096]{1,0:T(8,128)(2,1)}, f32[256,512]{1,0:T(8,128)}) custom-call(s32[16]{0:T(128)S(4)} %get-tuple-element.10.order, bf16[256,512]{1,0:T(8,128)(2,1)S(1)} %get-tuple-element.11.key, bf16[16,256,256]{2,1,0:T(8,128)(2,1)S(1)} %get-tuple-element.12.ig, f32[256,512]{1,0:T(8,128)S(1)} %get-tuple-element.13.gb), custom_call_target="tpu_custom_call" | custom-call | tf_op jit(solution)/shard_map/pallas_call | solution.py:750
